TPU v7x, 256 devices: a whole 4x4x8 slice. The times are simulated.
256 devices in a mesh: data: 256 (over z, y, x, core).
Axes of the slice: x: 4, y: 4, z: 8, core: 2. Of those that a mesh axis runs over, the one named last changes fastest.
Arguments:
- view_one: bfloat16 [65536, 256], P('data')
- view_two: bfloat16 [65536, 256], P('data')
- protos: bfloat16 [1024, 256], replicated
- valid_mask: int32 [65536], P('data')
Outputs:
- output 1: float32 [65536, 1024], P('data')
- output 2: float32 [65536, 1024], P('data')
- output 3: float32 [], replicated
- output 4: float32 [65536, 256], P('data')
- output 5: float32 [65536, 256], P('data')
- output 6: float32 [1024, 256], replicated
All inputs are finite; a program needn't handle non-finite values.
Results may differ from a plain program's by a relative error of at most 0.001.
Values are sent between devices in bfloat16 or wider.
A program may use at most 768 MiB of HBM per device.

v0:
```python
import jax
import jax.numpy as jnp
from jax import lax
from jax.sharding import PartitionSpec as P

SINK_EPS = 0.05
SOFT_TEMP = 0.1
SINK_ITERS = 3


def solution(mesh):
    def value_a14(scores, weights, valid_count):
        proto_count = scores.shape[1]
        transport = jnp.exp(scores / SINK_EPS) * weights
        for sweep_idx in range(SINK_ITERS):
            col_sum = lax.psum(jnp.sum(transport, axis=0, keepdims=True), "data")
            transport = transport / (proto_count * col_sum)
            row_sum = jnp.sum(transport, axis=1, keepdims=True) + (1.0 - weights)
            transport = transport / (valid_count * row_sum)
        return transport * valid_count

    def local_step(view_one, view_two, protos, valid_mask):
        weights = valid_mask.astype(jnp.float32)[:, None]
        valid_count = lax.psum(jnp.sum(weights), "data")
        score_one = jnp.einsum("nd,kd->nk", view_one, protos, preferred_element_type=jnp.float32)
        codes_one = value_a14(score_one, weights, valid_count)
        score_two = jnp.einsum("nd,kd->nk", view_two, protos, preferred_element_type=jnp.float32)
        codes_two = value_a14(score_two, weights, valid_count)
        logp_one = jax.nn.log_softmax(score_one / SOFT_TEMP, axis=1)
        logp_two = jax.nn.log_softmax(score_two / SOFT_TEMP, axis=1)
        part_loss = -(jnp.sum(codes_two * logp_one) + jnp.sum(codes_one * logp_two))
        loss_value = lax.psum(part_loss, "data") / (2.0 * valid_count)
        grad_scale = weights / (2.0 * valid_count * SOFT_TEMP)
        grad_one = ((jnp.exp(logp_one) - codes_two) * grad_scale).astype(jnp.bfloat16)
        grad_two = ((jnp.exp(logp_two) - codes_one) * grad_scale).astype(jnp.bfloat16)
        dz_one = jnp.dot(grad_one, protos, preferred_element_type=jnp.float32)
        dz_two = jnp.dot(grad_two, protos, preferred_element_type=jnp.float32)
        part_grad = (jnp.einsum("nk,nd->kd", grad_one, view_one, preferred_element_type=jnp.float32)
                     + jnp.einsum("nk,nd->kd", grad_two, view_two, preferred_element_type=jnp.float32))
        d_protos = lax.psum(part_grad, "data")
        return codes_one, codes_two, loss_value, dz_one, dz_two, d_protos

    return jax.shard_map(
        local_step,
        mesh=mesh,
        in_specs=(P("data", None), P("data", None), P(None, None), P("data")),
        out_specs=(P("data", None), P("data", None), P(), P("data", None), P("data", None), P(None, None)),
        check_vma=False,
    )
```

profile of v0, /device:TPU:1, one launch (start us, length us, event | category | flops | bytes accessed | tf_op | source)
XLA Modules:
  0.0 672.5 jit_solution(9547906263502663116)
XLA Ops:
  7.2 0.7 convert_element_type.9
  8.0 0.6 convert_reduce_fusion
  8.6 1.4 multiply_reduce_fusion.2
  9.9 0.5 multiply_reduce_fusion.3
  10.5 81.5 %all-reduce.1 = (f32[]{:T(128)}, f32[1,1024]{1,0:T(1,128)S(1)}) all-reduce(f32[]{:T(128)} %convert_reduce_fusion, f32[1,1024]{1,0:T(1,128)S(1)} %bitcast.53), channel_id=1, replica_groups=mesh['data'=256] {'data'}, use_global_device_ids=true, to_apply=%region_3.0 | all-reduce | flops 1025 | bytes 8200 | tf_op jit(solution)/shard_map/psum | solution.py:24
  92.0 0.5 exponential_reduce_fusion.1
  92.5 0.7 add_multiply_fusion.5
  93.2 0.7 exponential_reduce_fusion
  93.9 72.4 %psum.65 = f32[1,1024]{1,0:T(1,128)S(1)} all-reduce(f32[1,1024]{1,0:T(1,128)S(1)} %bitcast.49), channel_id=1, replica_groups=mesh['data'=256] {'data'}, use_global_device_ids=true, to_apply=%region_6.0 | all-reduce | flops 1024 | bytes 8192 | tf_op jit(solution)/shard_map/psum | solution.py:16
  166.3 0.5 fusion.19
  166.7 0.7 add_multiply_fusion.4
  167.8 73.8 %all-reduce = (f32[1,1024]{1,0:T(1,128)S(1)}, f32[1,1024]{1,0:T(1,128)S(1)}) all-reduce(f32[1,1024]{1,0:T(1,128)S(1)} %bitcast.50, f32[1,1024]{1,0:T(1,128)S(1)} %bitcast.48), channel_id=1, replica_groups=mesh['data'=256] {'data'}, use_global_device_ids=true, to_apply=%region_9.0 | all-reduce | flops 2048 | bytes 16384 | tf_op jit(solution)/shard_map/psum | solution.py:16
  241.6 0.5 fusion.23
  242.8 0.7 add_multiply_fusion.3
  243.4 2.2 multiply_convert_fusion
  245.6 1.1 multiply_reduce_fusion
  246.7 0.7 add_multiply_fusion.2
  247.7 73.4 %psum.68 = f32[1,1024]{1,0:T(1,128)S(1)} all-reduce(f32[1,1024]{1,0:T(1,128)S(1)} %bitcast.51), channel_id=1, replica_groups=mesh['data'=256] {'data'}, use_global_device_ids=true, to_apply=%region_15.0 | all-reduce | flops 1024 | bytes 8192 | tf_op jit(solution)/shard_map/psum | solution.py:16
  321.2 0.5 fusion.18
  321.6 0.7 add_multiply_fusion.1
  322.7 74.4 %psum.69 = f32[1,1024]{1,0:T(1,128)S(1)} all-reduce(f32[1,1024]{1,0:T(1,128)S(1)} %bitcast.52), channel_id=1, replica_groups=mesh['data'=256] {'data'}, use_global_device_ids=true, to_apply=%region_18.0 | all-reduce | flops 1024 | bytes 8192 | tf_op jit(solution)/shard_map/psum | solution.py:16
  397.1 0.5 fusion.22
  397.6 0.7 add_multiply_fusion
  398.3 2.3 multiply_convert_fusion.1
  401.0 0.7 copy-done.1
  401.7 1.3 convolution_add_fusion
  403.0 2.2 multiply_reduce_fusion.1
  406.6 73.8 %psum.70 = f32[]{:T(128)} all-reduce(f32[]{:T(128)S(6)} %neg.3), channel_id=1, replica_groups=mesh['data'=256] {'data'}, use_global_device_ids=true, to_apply=%region_24.0 | all-reduce | flops 1 | bytes 8 | tf_op jit(solution)/shard_map/psum | solution.py:32
  481.7 1.0 fusion.28
  482.7 1.0 fusion.29
  483.7 178.6 %all-reduce.4.cloned.1.call-done = f32[1024,256]{1,0:T(8,128)} async-done(((f32[1024,256]{1,0:T(8,128)}), f32[1024,256]{1,0:T(8,128)}) %all-reduce.4.cloned.1.call-update) | async-done | bytes 1048592 | tf_op jit(solution)/shard_map/psum | solution.py:40
  662.3 2.3 copy.11
  (24 shorter events, 1.6 us)
Async XLA Ops:
  7.2 1.4 copy-start
  7.2 0.8 copy-start.5
  7.2 655.1 %all-reduce.4.cloned.1.call-start = ((), (), s32[]{:S(2)}) async-start(), calls=%async_computation | async-start | bytes 2097152 | tf_op jit(solution)/shard_map/psum | solution.py:40
  8.6 1.4 copy-start.4
  245.6 1.1 copy-start.2
  400.6 1.0 copy-start.1
  400.6 1.1 copy-start.3
Sparse Core Ops, SparseCore 0:
  403.2 259.0 all-reduce.3
where the time goes:
time: 674 us; the launch traced here: 673 us
  blocking collectives  449 us (67%)
  waiting for transfers between devices  179 us (27%)
  between operations  18.6 us (3%)
  other arithmetic  17.5 us (3%)
    psum x4, blocking collectives, value_a14(): col_sum = lax.psum(jnp.sum(transport, axis=0, keepdims=True), 'data')  294 us
    psum x1, waiting for transfers between devices, local_step(): d_protos = lax.psum(part_grad, 'data')  179 us
    psum x1, blocking collectives, local_step(): valid_count = lax.psum(jnp.sum(weights), 'data')  81.5 us
    psum x1, blocking collectives, local_step(): loss_value = lax.psum(part_loss, 'data') / (2.0 * valid_count)  73.8 us
  transfers between devices with their start and end apart: 1, of which 1 were waited for; matrix products, arithmetic and copies ran while one was open for 1% of the time, Pallas kernels for 0%

commit v1 on v0

v1 whole, which is shorter than its diff:
```python
import functools

import jax
import jax.numpy as jnp
from jax import lax
from jax.experimental import pallas as pl
from jax.experimental.pallas import tpu as pltpu
from jax.sharding import PartitionSpec as P

MESH = pl.DeviceIdType.MESH
F32 = jnp.float32
BF16 = jnp.bfloat16
INV_TEMP = 10.0
LANES = 128


def torus(devices):
    return {256: (4, 4, 8), 16: (2, 2, 2)}[devices]


class Place:
    def __init__(self, dims):
        nx, ny, nz = dims
        self.np, self.nz = nx * ny, nz
        me = lax.axis_index("data")
        self.core = lax.rem(me, 2)
        self.p = lax.rem(me // 2, self.np)
        self.z = me // (2 * self.np)
        x, y = lax.rem(self.p, nx), self.p // nx

        def ring(d, n):
            return min(d, n - d)

        steps = [(dx, dy) for dy in range(ny) for dx in range(nx) if dx or dy]
        steps.sort(key=lambda s: -(ring(s[0], nx) + ring(s[1], ny)))
        self.plane_p = [lax.rem(y + dy, ny) * nx + lax.rem(x + dx, nx) for dx, dy in steps]
        self.plane = [self.at(self.z, p, self.core) for p in self.plane_p]
        dzs = sorted(range(1, nz), key=lambda d: -ring(d, nz))
        self.column_z = [lax.rem(self.z + d, nz) for d in dzs]
        self.column = [self.at(z, self.p, self.core) for z in self.column_z]
        self.column_other = [self.at(z, self.p, 1 - self.core) for z in self.column_z]
        self.partner = self.at(self.z, self.p, 1 - self.core)

    def at(self, z, p, core):
        return (z * self.np + p) * 2 + core

    def far_first(self, j):
        half = self.nz // 2
        d = jnp.where(lax.rem(j, 2) == 1, half - (j + 1) // 2, half + j // 2)
        return lax.rem(self.z + d, self.nz)


def send(src, dst, send_sem, recv_sem, device):
    copy = pltpu.make_async_remote_copy(
        src_ref=src, dst_ref=dst, send_sem=send_sem, recv_sem=recv_sem, device_id=(device,), device_id_type=MESH
    )
    copy.start()
    return copy


def wait_bytes(ref, sem):
    pltpu.make_async_copy(ref, ref, sem).wait()


def enter(devices):
    barrier = pltpu.get_barrier_semaphore()
    for device in devices:
        pl.semaphore_signal(barrier, inc=1, device_id=(device,), device_id_type=MESH)


def entered(devices):
    pl.semaphore_wait(pltpu.get_barrier_semaphore(), len(devices))


def column_of(row):
    return jnp.transpose(jnp.broadcast_to(row, (LANES, LANES)))[:, :1]


def sinkhorn_kernel(dims, z1_ref, z2_ref, c_ref, m_ref, out_ref, zs, ms, mcol, plan, xyb, zb, zlast,
                    pair_send, pair_recv, xy_send, xy_recv, z_send, z_recv):
    here = Place(dims)
    rows, protos = z1_ref.shape[0], c_ref.shape[0]
    groups = here.plane + here.column + here.column_other + [here.partner]
    enter(groups)
    first = here.core == 0

    zs[0:rows, :] = jnp.where(first, z1_ref[...], z2_ref[...])
    for h in range(rows // LANES):
        mcol[h * LANES:(h + 1) * LANES, :] = column_of(m_ref[h:h + 1, :].astype(F32))

    def fill(i, acc):
        at = pl.ds(pl.multiple_of(i * LANES, LANES), LANES)
        s = lax.dot_general(zs[at, :], c_ref[...], (((1,), (1,)), ((), ())), preferred_element_type=F32)
        e = jnp.exp(s * INV_TEMP)
        e = e * e
        plan[at, :] = e
        return acc + jnp.sum((e * mcol[at, :]).reshape(LANES // 8, 8, protos), axis=0)

    acc = lax.fori_loop(0, rows // LANES, fill, jnp.zeros((8, protos), F32))

    entered(groups)

    @pl.when(first)
    def _():
        send(z2_ref, zs.at[pl.ds(rows, rows)], pair_send.at[0], pair_recv.at[0], here.partner)

    @pl.when(jnp.logical_not(first))
    def _():
        send(z1_ref, zs.at[pl.ds(rows, rows)], pair_send.at[0], pair_recv.at[0], here.partner)

    mask_copy = send(m_ref, ms, pair_send.at[1], pair_recv.at[1], here.partner)
    mask_copy.wait()
    for h in range(rows // LANES):
        mcol[rows + h * LANES:rows + (h + 1) * LANES, :] = column_of(ms[h:h + 1, :].astype(F32))
    count = jnp.sum((m_ref[...] + ms[...]).astype(F32), keepdims=True)
    wait_bytes(zs.at[pl.ds(rows, rows)], pair_recv.at[0])
    wait_bytes(zs.at[pl.ds(0, rows)], pair_send.at[0])
    acc = lax.fori_loop(rows // LANES, 2 * rows // LANES, fill, acc)

    def chunk_sum(acc):
        return jnp.sum(acc, axis=0, keepdims=True)

    sent = []

    def all_sum(t, value, last):
        xyb[t, here.p] = jnp.concatenate([value, jnp.broadcast_to(count, (1, LANES))], axis=1)
        mine = xyb.at[t, here.p]
        for i, device in enumerate(here.plane):
            sent.append(send(mine, mine, xy_send.at[t, i], xy_recv.at[t], device))
        wait_bytes(xyb.at[t, pl.ds(0, here.np - 1)], xy_recv.at[t])
        part = jnp.sum(xyb[t], axis=0)
        if not last:
            zb[t, here.z] = part
            mine = zb.at[t, here.z]
            for i, device in enumerate(here.column):
                sent.append(send(mine, mine, z_send.at[t, i], z_recv.at[t], device))
            wait_bytes(zb.at[t, pl.ds(0, here.nz - 1)], z_recv.at[t])
            return jnp.sum(zb[t], axis=0)[:, :protos]
        slot = here.core * here.nz + here.z
        zlast[slot] = part
        mine = zlast.at[slot]
        targets = here.column + here.column_other + [here.partner]
        for i, device in enumerate(targets):
            sent.append(send(mine, mine, z_send.at[t, i], z_recv.at[t], device))
        wait_bytes(zlast.at[pl.ds(0, 2 * here.nz - 1)], z_recv.at[t])
        for view in range(2):
            out_ref[view] = jnp.sum(zlast[view * here.nz:(view + 1) * here.nz], axis=0)
        return None

    def sweep(a):
        step = 32

        def body(i, acc):
            at = pl.ds(pl.multiple_of(i * step, step), step)
            e = plan[at, :]
            m = mcol[at, :]
            r = jnp.sum(e * a, axis=1, keepdims=True) * m + (1.0 - m)
            return acc + jnp.sum((e * (m / r)).reshape(step // 8, 8, protos), axis=0)

        return lax.fori_loop(0, 2 * rows // step, body, jnp.zeros((8, protos), F32), unroll=2)

    for t in range(3):
        total = all_sum(t, chunk_sum(acc), t == 2)
        if t < 2:
            acc = sweep(1.0 / (protos * total))
    for copy in sent:
        copy.wait_send()


def sinkhorn_columns(dims, view_one, view_two, protos, mask):
    rows, depth = view_one.shape
    count = protos.shape[0]
    width = count + LANES
    n_plane, n_z = dims[0] * dims[1], dims[2]
    vmem = pl.BlockSpec(memory_space=pltpu.VMEM)
    return pl.pallas_call(
        functools.partial(sinkhorn_kernel, dims),
        out_shape=jax.ShapeDtypeStruct((2, 1, width), F32),
        in_specs=[vmem] * 4,
        out_specs=vmem,
        scratch_shapes=[
            pltpu.VMEM((2 * rows, depth), BF16),
            pltpu.VMEM((rows // LANES, LANES), jnp.int32),
            pltpu.VMEM((2 * rows, 1), F32),
            pltpu.VMEM((2 * rows, count), F32),
            pltpu.VMEM((3, n_plane, 1, width), F32),
            pltpu.VMEM((2, n_z, 1, width), F32),
            pltpu.VMEM((2 * n_z, 1, width), F32),
            pltpu.SemaphoreType.DMA((2,)),
            pltpu.SemaphoreType.DMA((2,)),
            pltpu.SemaphoreType.DMA((3, n_plane - 1)),
            pltpu.SemaphoreType.DMA((3,)),
            pltpu.SemaphoreType.DMA((3, 2 * n_z - 1)),
            pltpu.SemaphoreType.DMA((3,)),
        ],
        compiler_params=pltpu.CompilerParams(collective_id=0, has_side_effects=True),
        name="sinkhorn",
    )(view_one, view_two, protos, mask.reshape(rows // LANES, LANES))


def reduce_kernel(dims, part_ref, loss_ref, out_ref, loss_out, part, inbox, half, rs, tot, zrs, full,
                  lpair, lxy, lz, c_send, c_recv, r_send, r_recv, t_send, t_recv,
                  g_send, g_recv, x_send, x_recv, d_send, d_recv, l_send, l_recv):
    here = Place(dims)
    n_plane, n_z = here.np, here.nz
    chunk = part.shape[3]
    groups = here.plane + here.column + [here.partner]
    enter(groups)
    for h in range(2):
        part[h] = part_ref[:, h * LANES:(h + 1) * LANES].reshape(n_z, n_plane, chunk, LANES)
    lpair[here.core] = loss_ref[...]
    entered(groups)

    sent = []
    lmine = lpair.at[here.core]
    sent.append(send(lmine, lmine, l_send.at[0], l_recv.at[0], here.partner))

    other = 1 - here.core

    def give(j, _):
        z = here.far_first(j)
        send(part.at[other, z], inbox.at[z], c_send.at[j], c_recv.at[j], here.partner)
        return 0

    lax.fori_loop(0, n_z, give, 0)

    def spread(j, _):
        z = here.far_first(j)
        wait_bytes(inbox.at[z], c_recv.at[j])
        half[z] = part[here.core, z] + inbox[z]
        rs[here.p, z] = half[z, here.p]
        for i in range(n_plane - 1):
            send(half.at[z, here.plane_p[i]], rs.at[here.p, z], r_send.at[j, i], r_recv.at[j], here.plane[i])
        return 0

    lax.fori_loop(0, n_z, spread, 0)

    wait_bytes(lpair.at[0], l_recv.at[0])
    lxy[here.p] = lpair[0] + lpair[1]
    lmine = lxy.at[here.p]
    for i, device in enumerate(here.plane):
        sent.append(send(lmine, lmine, l_send.at[1 + i], l_recv.at[1], device))

    def gather(j, _):
        z = here.far_first(j)
        wait_bytes(rs.at[pl.ds(0, n_plane - 1), z], r_recv.at[j])
        tot[z] = jnp.sum(rs[:, z], axis=0)

        @pl.when(j < n_z - 1)
        def _():
            send(tot.at[z], zrs.at[here.z], t_send.at[j], t_recv.at[0], here.at(z, here.p, here.core))

        return 0

    lax.fori_loop(0, n_z, gather, 0)
    wait_bytes(lxy.at[pl.ds(0, n_plane - 1)], l_recv.at[1])
    lz[here.z] = jnp.sum(lxy[...], axis=0)
    lmine = lz.at[here.z]
    for i, device in enumerate(here.column):
        sent.append(send(lmine, lmine, l_send.at[n_plane + i], l_recv.at[2], device))

    zrs[here.z] = tot[here.z]
    wait_bytes(zrs.at[pl.ds(0, n_z - 1)], t_recv.at[0])
    full[here.core, here.z, here.p] = jnp.sum(zrs[...], axis=0)

    def near_first(j):
        return here.far_first(n_z - 1 - j)

    mine = full.at[here.core, here.z, here.p]
    for i, device in enumerate(here.column):
        sent.append(send(mine, mine, g_send.at[i], g_recv.at[here.z], device))

    def forward(j, _):
        z = near_first(j)
        held = full.at[here.core, z, here.p]

        @pl.when(j > 0)
        def _():
            wait_bytes(held, g_recv.at[z])

        for i in range(n_plane - 1):
            send(held, held, x_send.at[j, i], x_recv.at[j], here.plane[i])
        return 0

    lax.fori_loop(0, n_z, forward, 0)

    def cross(j, _):
        z = near_first(j)
        wait_bytes(full.at[here.core, z, pl.ds(0, n_plane - 1)], x_recv.at[j])
        held = full.at[here.core, z]
        send(held, held, d_send.at[j], d_recv.at[j], here.partner)
        return 0

    lax.fori_loop(0, n_z, cross, 0)

    wait_bytes(lz.at[pl.ds(0, n_z - 1)], l_recv.at[2])
    loss_out[...] = jnp.sum(lz[...], axis=0)

    def finish(j, _):
        z = near_first(j)
        wait_bytes(full.at[other, z], d_recv.at[j])
        wait_bytes(full.at[here.core, z], d_send.at[j])
        wait_bytes(inbox.at[z], c_send.at[j])

        @pl.when(j < n_z - 1)
        def _():
            wait_bytes(tot.at[z], t_send.at[j])

        for i in range(n_plane - 1):
            wait_bytes(tot.at[z], r_send.at[j, i])
            wait_bytes(tot.at[z], x_send.at[j, i])
        return 0

    lax.fori_loop(0, n_z, finish, 0)
    for h in range(2):
        out_ref[:, h * LANES:(h + 1) * LANES] = full[h].reshape(n_z * n_plane * chunk, LANES)
    for copy in sent:
        copy.wait_send()


def reduce_all(dims, part, loss_row):
    count, depth = part.shape
    n_plane, n_z = dims[0] * dims[1], dims[2]
    chunk = count // (n_plane * n_z)
    vmem = pl.BlockSpec(memory_space=pltpu.VMEM)
    dma = pltpu.SemaphoreType.DMA
    return pl.pallas_call(
        functools.partial(reduce_kernel, dims),
        out_shape=(jax.ShapeDtypeStruct((count, depth), F32), jax.ShapeDtypeStruct((1, LANES), F32)),
        in_specs=[vmem] * 2,
        out_specs=(vmem, vmem),
        scratch_shapes=[
            pltpu.VMEM((2, n_z, n_plane, chunk, LANES), F32),
            pltpu.VMEM((n_z, n_plane, chunk, LANES), F32),
            pltpu.VMEM((n_z, n_plane, chunk, LANES), F32),
            pltpu.VMEM((n_plane, n_z, chunk, LANES), F32),
            pltpu.VMEM((n_z, chunk, LANES), F32),
            pltpu.VMEM((n_z, chunk, LANES), F32),
            pltpu.VMEM((2, n_z, n_plane, chunk, LANES), F32),
            pltpu.VMEM((2, 1, LANES), F32),
            pltpu.VMEM((n_plane, 1, LANES), F32),
            pltpu.VMEM((n_z, 1, LANES), F32),
            dma((n_z,)), dma((n_z,)),
            dma((n_z, n_plane - 1)), dma((n_z,)),
            dma((n_z,)), dma((1,)),
            dma((n_z - 1,)), dma((n_z,)),
            dma((n_z, n_plane - 1)), dma((n_z,)),
            dma((n_z,)), dma((n_z,)),
            dma((n_plane + n_z,)), dma((3,)),
        ],
        compiler_params=pltpu.CompilerParams(collective_id=1, has_side_effects=True),
        name="reduce_all",
    )(part, loss_row)


def solution(mesh):
    dims = torus(mesh.size)

    def local_step(view_one, view_two, protos, valid_mask):
        sums = sinkhorn_columns(dims, view_one, view_two, protos, valid_mask)
        count = protos.shape[0]
        valid_count = sums[0, 0, count]
        weights = valid_mask.astype(F32)[:, None]

        def scores(view):
            return jnp.einsum("nd,kd->nk", view, protos, preferred_element_type=F32) * INV_TEMP

        def codes(score, v):
            e = jnp.exp(score)
            a = 1.0 / (count * sums[v, :, :count])
            plan = e * e * a
            return plan * (weights / (weights * jnp.sum(plan, axis=1, keepdims=True) + (1.0 - weights)))

        s1, s2 = scores(view_one), scores(view_two)
        q1, q2 = codes(s1, 0), codes(s2, 1)
        logp1 = s1 - jnp.log(jnp.sum(jnp.exp(s1), axis=1, keepdims=True))
        logp2 = s2 - jnp.log(jnp.sum(jnp.exp(s2), axis=1, keepdims=True))
        part_loss = -(jnp.sum(q2 * logp1) + jnp.sum(q1 * logp2)) / (2.0 * valid_count)
        scale = weights * (0.5 * INV_TEMP) / valid_count
        g1 = ((jnp.exp(logp1) - q2) * scale).astype(BF16)
        g2 = ((jnp.exp(logp2) - q1) * scale).astype(BF16)
        dz1 = jnp.dot(g1, protos, preferred_element_type=F32)
        dz2 = jnp.dot(g2, protos, preferred_element_type=F32)
        part = (jnp.einsum("nk,nd->kd", g1, view_one, preferred_element_type=F32)
                + jnp.einsum("nk,nd->kd", g2, view_two, preferred_element_type=F32))
        d_protos, loss_row = reduce_all(dims, part, jnp.broadcast_to(part_loss, (1, LANES)))
        return q1, q2, loss_row[0, 0], dz1, dz2, d_protos

    return jax.shard_map(
        local_step,
        mesh=mesh,
        in_specs=(P("data", None), P("data", None), P(None, None), P("data")),
        out_specs=(P("data", None), P("data", None), P(), P("data", None), P("data", None), P(None, None)),
        check_vma=False,
    )
```

time: 674 us -> 98.2 us (0.15)
  blocking collectives: 449 us -> 0 us
  waiting for transfers between devices: 179 us -> 0 us
  Pallas kernels: 0 us -> 79.3 us
  between operations: 18.6 us -> 3.93 us
  other arithmetic: 17.5 us -> 4.3 us
    psum x6 -> x0, blocking collectives: 449 us -> none  [the longest x4 294 us: value_a14(): col_sum = lax.psum(jnp.sum(transport, axis=0, keepdims=True), 'data')]
    psum x1 -> x0, waiting for transfers between devices: 179 us -> none  [local_step(): d_protos = lax.psum(part_grad, 'data')]
    pallas_call x0 -> x2, Pallas kernels: none -> 79.3 us  [the longest x1 46 us: sinkhorn_columns(): pl.pallas_call(functools.partial(sinkhorn_kernel, dims), out_shape=jax.Sh...]
  transfers between devices with their start and end apart: 1 -> 0, of which waited for: 1 -> 0; matrix products, arithmetic and copies ran while one was open for 1% -> 0% of each run, Pallas kernels for 0% -> 0%
where the time goes in v1:
time: 98.2 us; the launch traced here: 97.9 us
  Pallas kernels  79.3 us (81%)
  local copies, waits for them, and re-layouts  5.72 us (6%)
  matrix products  4.65 us (5%)
  other arithmetic  4.3 us (4%)
  between operations  3.93 us (4%)
    pallas_call x1, Pallas kernels, sinkhorn_columns(): pl.pallas_call(functools.partial(sinkhorn_kernel, dims), out_shape=jax.Sh...  46 us
    pallas_call x1, Pallas kernels, reduce_all(): pl.pallas_call(functools.partial(reduce_kernel, dims), out_shape=(jax.Sha...  33.3 us
    unnamed x15, local copies, waits for them, and re-layouts  4.08 us

profile of v1, /device:TPU:1, one launch (start us, length us, event | category | flops | bytes accessed | tf_op | source)
XLA Modules:
  0.0 97.9 jit_solution(17770687327176837811)
XLA Ops:
  0.6 0.0 copy-start
  0.6 0.0 copy-start.3
  0.7 46.0 %sinkhorn.1 = f32[2,1,1152]{2,1,0:T(1,128)} custom-call(bf16[256,256]{1,0:T(8,128)(2,1)} %z1_ref.1, bf16[256,256]{1,0:T(8,128)(2,1)} %z2_ref.1, bf16[1024,256]{1,0:T(8,128)(2,1)} %c_ref.1, s32[2,128]{1,0:T(2,128)} %bitcast.22), custom_call_target="tpu_custom_call" | custom-call | tf_op jit(solution)/shard_map/sinkhorn/pallas_call | solution.py:176
  46.6 1.1 %slice.14 = f32[1,1,1]{2,1,0:T(1,128)} slice(f32[2,1,1152]{2,1,0:T(1,128)} %sinkhorn.1), slice={[0:1], [0:1], [1024:1025]} | slice | bytes 8 | tf_op jit(solution)/shard_map/slice | solution.py:362
  48.4 0.7 multiply_divide_fusion
  49.1 0.0 copy-done
  49.1 0.0 copy-done.3
  49.1 0.0 copy-start.4
  49.1 0.4 exponential_reduce_fusion
  49.6 0.5 copy-done.4
  50.0 0.5 exponential_reduce_fusion.1
  50.6 0.0 copy-start.5
  50.6 0.7 copy-done.5
  51.3 0.7 add_divide_fusion.1
  51.9 0.4 multiply_convert_fusion
  52.3 0.0 copy-start.1
  52.4 1.1 %multiply_reduce_fusion = (f32[]{:T(128)}, f32[256]{0:T(256)S(1)}) fusion(f32[256,1024]{1,0:T(8,128)S(1)} %get-tuple-element.31, f32[256,1024]{1,0:T(8,128)S(1)} %get-tuple-element.23, f32[256]{0:T(256)S(1)} %log.17, f32[1024]{0:T(1024)S(1)} %bitcast.18), kind=kLoop, calls=%fused_computation.3 | loop fusion | flops 1572607 | bytes 2103300 | tf_op jit(solution)/shard_map/reduce_sum | solution.py:378
  53.5 0.0 copy-done.1
  53.5 1.1 %multiply_reduce_fusion.1 = (f32[]{:T(128)}, f32[256,1024]{1,0:T(8,128)S(1)}) fusion(f32[256,1024]{1,0:T(8,128)S(1)} %get-tuple-element.24, f32[256]{0:T(256)S(1)} %log.16, f32[256]{0:T(256)S(1)} %add_divide_fusion, f32[1024]{0:T(1024)S(1)} %bitcast.19, f32[256,1024]{1,0:T(8,128)S(1)} %get-tuple-element.23), kind=kLoop, calls=%fused_computation.4 | loop fusion | flops 1572863 | bytes 3151876 | tf_op jit(solution)/shard_map/reduce_sum | solution.py:378
  54.6 0.0 copy-start.2
  56.0 0.3 multiply_convert_fusion.1
  56.2 0.0 copy-done.2
  56.2 0.5 broadcast_in_dim.2.loss_ref
  56.8 1.0 %fusion.7 = f32[256,256]{1,0:T(8,128)} fusion(bf16[256,1024]{1,0:T(8,128)(2,1)S(1)} %multiply_convert_fusion.1, bf16[1024,256]{1,0:T(8,128)(2,1)S(1)} %copy-done), kind=kOutput, calls=%fused_computation.22 | convolution fusion | flops 134217728 | bytes 1310720 | tf_op jit(solution)/shard_map/dot_general | solution.py:382
  57.8 1.0 %fusion.8 = f32[256,256]{1,0:T(8,128)} fusion(bf16[256,1024]{1,0:T(8,128)(2,1)S(1)} %get-tuple-element.16, bf16[1024,256]{1,0:T(8,128)(2,1)S(1)} %copy-done), kind=kOutput, calls=%fused_computation.23 | convolution fusion | flops 134217728 | bytes 1310720 | tf_op jit(solution)/shard_map/dot_general | solution.py:383
  58.8 0.4 fusion.6
  59.1 1.3 %convolution_add_fusion.part_ref = f32[1024,256]{1,0:T(8,128)} fusion(f32[1024,256]{1,0:T(8,128)S(1)} %fusion.6, bf16[256,1024]{1,0:T(8,128)(2,1)S(1)} %get-tuple-element.16, bf16[256,256]{1,0:T(8,128)(2,1)S(1)} %copy-done.3), kind=kOutput, calls=%fused_computation | convolution fusion | flops 134479872 | bytes 2752512 | tf_op jit(solution)/shard_map/nk,nd->kd/dot_general | solution.py:385
  60.5 33.3 %reduce_all.1 = (f32[1024,256]{1,0:T(8,128)}, f32[1,128]{1,0:T(1,128)}) custom-call(f32[1024,256]{1,0:T(8,128)} %convolution_add_fusion.part_ref, f32[1,128]{1,0:T(1,128)} %broadcast_in_dim.2.loss_ref), custom_call_target="tpu_custom_call" | custom-call | tf_op jit(solution)/shard_map/reduce_all/pallas_call | solution.py:327
  93.8 0.0 copy-start.6
  93.8 0.7 copy-done.6
  94.5 2.3 %copy.13 = f32[1024,256]{1,0:T(8,128)} copy(f32[1024,256]{1,0:T(8,128)} %get-tuple-element.36) | data formatting | bytes 2097152
  (3 shorter events, 0.0 us)
Async XLA Ops:
  0.6 48.5 %copy-start = (bf16[1024,256]{1,0:T(8,128)(2,1)S(1)}, bf16[1024,256]{1,0:T(8,128)(2,1)}, u32[]{:S(2)}) copy-start(bf16[1024,256]{1,0:T(8,128)(2,1)} %c_ref.1) | copy-start | bytes 1572868
  0.6 48.5 %copy-start.3 = (bf16[256,256]{1,0:T(8,128)(2,1)S(1)}, bf16[256,256]{1,0:T(8,128)(2,1)}, u32[]{:S(2)}) copy-start(bf16[256,256]{1,0:T(8,128)(2,1)} %z2_ref.1) | copy-start | bytes 393220
  49.1 0.9 copy-start.4
  50.6 0.7 copy-start.5
  52.3 1.1 %copy-start.1 = (f32[256,1024]{1,0:T(8,128)}, f32[256,1024]{1,0:T(8,128)S(1)}, u32[]{:S(2)}) copy-start(f32[256,1024]{1,0:T(8,128)S(1)} %get-tuple-element.31) | copy-start | bytes 3145732
  54.6 1.6 %copy-start.2 = (f32[256,1024]{1,0:T(8,128)}, f32[256,1024]{1,0:T(8,128)S(1)}, u32[]{:S(2)}) copy-start(f32[256,1024]{1,0:T(8,128)S(1)} %get-tuple-element.32) | copy-start | bytes 3145732
  93.8 0.7 copy-start.6

commit v2 on v1

v2 whole, which is shorter than its diff:
```python
import functools

import jax
import jax.numpy as jnp
from jax import lax
from jax.experimental import pallas as pl
from jax.experimental.pallas import tpu as pltpu
from jax.sharding import PartitionSpec as P

MESH = pl.DeviceIdType.MESH
F32 = jnp.float32
BF16 = jnp.bfloat16
INV_TEMP = 10.0
LANES = 128


def torus(devices):
    return {256: (4, 4, 8), 16: (2, 2, 2)}[devices]


class Place:
    def __init__(self, dims):
        nx, ny, nz = dims
        self.np, self.nz = nx * ny, nz
        me = lax.axis_index("data")
        self.core = lax.rem(me, 2)
        self.p = lax.rem(me // 2, self.np)
        self.z = me // (2 * self.np)
        x, y = lax.rem(self.p, nx), self.p // nx

        def ring(d, n):
            return min(d, n - d)

        steps = [(dx, dy) for dy in range(ny) for dx in range(nx) if dx or dy]
        steps.sort(key=lambda s: -(ring(s[0], nx) + ring(s[1], ny)))
        self.plane_p = [lax.rem(y + dy, ny) * nx + lax.rem(x + dx, nx) for dx, dy in steps]
        self.plane = [self.at(self.z, p, self.core) for p in self.plane_p]
        dzs = sorted(range(1, nz), key=lambda d: -ring(d, nz))
        self.column_z = [lax.rem(self.z + d, nz) for d in dzs]
        self.column = [self.at(z, self.p, self.core) for z in self.column_z]
        self.column_other = [self.at(z, self.p, 1 - self.core) for z in self.column_z]
        self.partner = self.at(self.z, self.p, 1 - self.core)

    def at(self, z, p, core):
        return (z * self.np + p) * 2 + core

    def far_first(self, j):
        half = self.nz // 2
        d = jnp.where(lax.rem(j, 2) == 1, half - (j + 1) // 2, half + j // 2)
        return lax.rem(self.z + d, self.nz)


def send(src, dst, send_sem, recv_sem, device):
    copy = pltpu.make_async_remote_copy(
        src_ref=src, dst_ref=dst, send_sem=send_sem, recv_sem=recv_sem, device_id=(device,), device_id_type=MESH
    )
    copy.start()
    return copy


def wait_bytes(ref, sem):
    pltpu.make_async_copy(ref, ref, sem).wait()


def enter(devices):
    barrier = pltpu.get_barrier_semaphore()
    for device in devices:
        pl.semaphore_signal(barrier, inc=1, device_id=(device,), device_id_type=MESH)


def entered(devices):
    pl.semaphore_wait(pltpu.get_barrier_semaphore(), len(devices))


def column_of(row):
    return jnp.transpose(jnp.broadcast_to(row, (LANES, LANES)))[:, :1]


def step_kernel(dims, z1_hbm, z2_hbm, c_hbm, m_hbm, q_out, dz_out, dc_out, loss_out,
                zin, cbuf, zx, m_own, ms, mcol, bcol, avec, plan, plan_other, prob, logp, grad, zt,
                xy_first, spare, xyb, z_first, zb, zlast, part, inbox, half, rs, tot, zrs, full, flip, lpair, lxy, lz,
                in_sem, pair_send, pair_recv, f_send, f_recv, xy_send, xy_recv, z_send, z_recv,
                c_send, c_recv, r_send, r_recv, t_send, t_recv,
                g_send, g_recv, x_send, x_recv, d_send, d_recv, l_send, l_recv):
    here = Place(dims)
    n_plane, n_z = here.np, here.nz
    rows, protos = zin.shape[1], cbuf.shape[0]
    block = protos // n_z
    mine, other = here.core, 1 - here.core
    plane_other = [here.at(here.z, p, other) for p in here.plane_p]
    groups = here.plane + plane_other + here.column + here.column_other + [here.partner]
    enter(groups)

    loads = [pltpu.make_async_copy(z1_hbm, zin.at[0], in_sem.at[0]),
             pltpu.make_async_copy(z2_hbm, zin.at[1], in_sem.at[1]),
             pltpu.make_async_copy(c_hbm, cbuf, in_sem.at[2]),
             pltpu.make_async_copy(m_hbm, m_own, in_sem.at[3])]
    for load in loads:
        load.start()
    loads[3].wait()
    mask = m_own[...].astype(F32)
    for h in range(rows // LANES):
        mcol[h * LANES:(h + 1) * LANES, :] = column_of(mask[h:h + 1, :])
    count = jnp.broadcast_to(jnp.sum(mask, keepdims=True), (1, LANES))
    for load in loads[:3]:
        load.wait()

    def scores(z):
        return lax.dot_general(z, cbuf[...], (((1,), (1,)), ((), ())), preferred_element_type=F32) * INV_TEMP

    def fold(e, m):
        return jnp.sum((e * m).reshape(LANES // 8, 8, protos), axis=0)

    def fill(i, accs):
        at = pl.ds(pl.multiple_of(i * LANES, LANES), LANES)
        out = []
        for view, plan_ref, acc in ((mine, plan, accs[0]), (other, plan_other, accs[1])):
            s = scores(zin[view, at, :])
            logp[view, at, :] = s
            e = jnp.exp(s)
            e = e * e
            plan_ref[at, :] = e
            out.append(acc + fold(e, mcol[at, :]))
        return tuple(out)

    zero = jnp.zeros((8, protos), F32)
    acc_mine, acc_other = lax.fori_loop(0, rows // LANES, fill, (zero, zero))

    def payload(acc):
        return jnp.concatenate([jnp.sum(acc, axis=0, keepdims=True), count], axis=1)

    sent = []
    slot = here.core * n_plane + here.p
    xy_first[slot] = payload(acc_mine)
    spare[...] = payload(acc_other)

    entered(groups)

    held = xy_first.at[slot]
    for i in range(n_plane - 1):
        sent.append(send(held, held, f_send.at[i], f_recv.at[0], here.plane[i]))
        sent.append(send(spare, held, f_send.at[n_plane + i], f_recv.at[0], plane_other[i]))
    sent.append(send(spare, held, f_send.at[n_plane - 1], f_recv.at[0], here.partner))
    sent.append(send(zin.at[other], zx, pair_send.at[0], pair_recv.at[0], here.partner))
    sent.append(send(m_own, ms, pair_send.at[1], pair_recv.at[1], here.partner))

    wait_bytes(ms, pair_recv.at[1])
    for h in range(rows // LANES):
        mcol[rows + h * LANES:rows + (h + 1) * LANES, :] = column_of(ms[h:h + 1, :].astype(F32))
    wait_bytes(zx, pair_recv.at[0])

    def fill_partner(i, _):
        e = jnp.exp(scores(zx[pl.ds(pl.multiple_of(i * LANES, LANES), LANES), :]))
        plan[pl.ds(pl.multiple_of(rows + i * LANES, LANES), LANES), :] = e * e
        return 0

    lax.fori_loop(0, rows // LANES, fill_partner, 0)

    def to_column(t, value, last):
        if not last:
            held = (z_first if t == 0 else zb).at[here.z]
            held[...] = value
            for i, device in enumerate(here.column):
                sent.append(send(held, held, z_send.at[t, i], z_recv.at[t], device))
            return
        slot = here.core * n_z + here.z
        zlast[slot] = value
        held = zlast.at[slot]
        for i, device in enumerate(here.column + here.column_other + [here.partner]):
            sent.append(send(held, held, z_send.at[t, i], z_recv.at[t], device))

    def from_column(t):
        buf = z_first if t == 0 else zb
        wait_bytes(buf.at[pl.ds(0, n_z - 1)], z_recv.at[t])
        return jnp.sum(buf[...], axis=0)

    def to_plane(t, value):
        xyb[t, here.p] = value
        held = xyb.at[t, here.p]
        for i, device in enumerate(here.plane):
            sent.append(send(held, held, xy_send.at[t, i], xy_recv.at[t], device))

    def from_plane(t):
        wait_bytes(xyb.at[t, pl.ds(0, n_plane - 1)], xy_recv.at[t])
        return jnp.sum(xyb[t], axis=0)

    def sweep(a):
        step = 32

        def body(i, acc):
            at = pl.ds(pl.multiple_of(i * step, step), step)
            e = plan[at, :]
            m = mcol[at, :]
            r = jnp.sum(e * a, axis=1, keepdims=True) * m + (1.0 - m)
            return acc + jnp.sum((e * (m / r)).reshape(step // 8, 8, protos), axis=0)

        acc = lax.fori_loop(0, 2 * rows // step, body, zero, unroll=2)
        return jnp.sum(acc, axis=0, keepdims=True)

    wait_bytes(xy_first.at[pl.ds(0, 2 * n_plane - 1)], f_recv.at[0])
    to_column(0, jnp.sum(xy_first[...], axis=0), False)

    def soften(i, _):
        at = pl.ds(pl.multiple_of(i * 32, 32), 32)
        for view in range(2):
            s = logp[view, at, :]
            s = s - jnp.log(jnp.sum(jnp.exp(s), axis=1, keepdims=True))
            logp[view, at, :] = s
            prob[view, at, :] = jnp.exp(s)
        return 0

    lax.fori_loop(0, rows // 32, soften, 0)
    for k, view in enumerate((mine, other)):
        zt[:, k * rows:(k + 1) * rows] = jnp.transpose(zin[view].astype(F32)).astype(BF16)

    total = from_column(0)
    valid = total[:, protos:]
    for t in (0, 1):
        a = 1.0 / (protos * total[:, :protos])
        to_plane(t, sweep(a))
        if t == 0:
            to_column(1, from_plane(0), False)
            total = from_column(1)
        else:
            to_column(2, from_plane(1), True)
    wait_bytes(zlast.at[pl.ds(0, 2 * n_z - 1)], z_recv.at[2])
    for view in range(2):
        avec[view] = 1.0 / (protos * jnp.sum(zlast[view * n_z:(view + 1) * n_z], axis=0))

    def weigh(i, _):
        at = pl.ds(pl.multiple_of(i * 32, 32), 32)
        m = mcol[at, :]
        for k, (view, plan_ref) in enumerate(((mine, plan), (other, plan_other))):
            r = jnp.sum(plan_ref[at, :] * avec[view], axis=1, keepdims=True) * m + (1.0 - m)
            bcol[k, at, :] = m / r
        return 0

    lax.fori_loop(0, rows // 32, weigh, 0)
    scale = mcol[0:rows, :] * (0.5 * INV_TEMP) / valid[:, :1]

    def derive(j, _):
        z = here.far_first(j)
        cols = pl.ds(pl.multiple_of(z * block, block), block)
        q_mine = plan[0:rows, cols] * avec[mine, :, cols] * bcol[0]
        q_other = plan_other[:, cols] * avec[other, :, cols] * bcol[1]
        q_out[mine, :, cols] = q_mine
        q_out[other, :, cols] = q_other
        g = jnp.concatenate([((prob[mine, :, cols] - q_other) * scale).astype(BF16),
                             ((prob[other, :, cols] - q_mine) * scale).astype(BF16)], axis=0)
        grad[:, cols] = g
        d = lax.dot_general(zt[...], g, (((1,), (0,)), ((), ())), preferred_element_type=F32)
        part[z] = d.reshape(part.shape[1:])
        send(part.at[z, other], inbox.at[z], c_send.at[j], c_recv.at[j], here.partner)
        return 0

    lax.fori_loop(0, n_z, derive, 0)

    def spread(j, _):
        z = here.far_first(j)
        wait_bytes(inbox.at[z], c_recv.at[j])
        half[z] = part[z, mine] + inbox[z]
        rs[here.p, z] = half[z, here.p]
        for i in range(n_plane - 1):
            send(half.at[z, here.plane_p[i]], rs.at[here.p, z], r_send.at[j, i], r_recv.at[j], here.plane[i])
        return 0

    lax.fori_loop(0, n_z, spread, 0)

    def lose(i, acc):
        at = pl.ds(pl.multiple_of(i * 32, 32), 32)
        pair = q_out[1, at, :] * logp[0, at, :] + q_out[0, at, :] * logp[1, at, :]
        return acc + jnp.sum(pair.reshape(4, 8, protos), axis=0)

    loss = jnp.sum(lax.fori_loop(0, rows // 32, lose, zero), keepdims=True)
    lpair[here.core] = jnp.broadcast_to(loss, (1, LANES)) * (-0.5) / valid
    lheld = lpair.at[here.core]
    sent.append(send(lheld, lheld, l_send.at[0], l_recv.at[0], here.partner))

    def descend(i, _):
        at = pl.ds(pl.multiple_of(i * LANES, LANES), LANES)
        for k, view in enumerate((mine, other)):
            g = grad[pl.ds(pl.multiple_of(k * rows + i * LANES, LANES), LANES), :]
            dz_out[view, at, :] = jnp.dot(g, cbuf[...], preferred_element_type=F32)
        return 0

    lax.fori_loop(0, rows // LANES, descend, 0)

    wait_bytes(lpair.at[0], l_recv.at[0])
    lxy[here.p] = lpair[0] + lpair[1]
    lheld = lxy.at[here.p]
    for i, device in enumerate(here.plane):
        sent.append(send(lheld, lheld, l_send.at[1 + i], l_recv.at[1], device))

    def gather(j, _):
        z = here.far_first(j)
        wait_bytes(rs.at[pl.ds(0, n_plane - 1), z], r_recv.at[j])
        tot[z] = jnp.sum(rs[:, z], axis=0)

        @pl.when(j < n_z - 1)
        def _():
            send(tot.at[z], zrs.at[here.z], t_send.at[j], t_recv.at[0], here.at(z, here.p, here.core))

        return 0

    lax.fori_loop(0, n_z, gather, 0)
    wait_bytes(lxy.at[pl.ds(0, n_plane - 1)], l_recv.at[1])
    lz[here.z] = jnp.sum(lxy[...], axis=0)
    lheld = lz.at[here.z]
    for i, device in enumerate(here.column):
        sent.append(send(lheld, lheld, l_send.at[n_plane + i], l_recv.at[2], device))

    zrs[here.z] = tot[here.z]
    wait_bytes(zrs.at[pl.ds(0, n_z - 1)], t_recv.at[0])
    full[here.z, here.p] = jnp.sum(zrs[...], axis=0)

    def near_first(j):
        return here.far_first(n_z - 1 - j)

    held = full.at[here.z, here.p]
    for i, device in enumerate(here.column):
        sent.append(send(held, held, g_send.at[i], g_recv.at[here.z], device))

    def forward(j, _):
        z = near_first(j)
        held = full.at[z, here.p]

        @pl.when(j > 0)
        def _():
            wait_bytes(held, g_recv.at[z])

        for i in range(n_plane - 1):
            send(held, held, x_send.at[j, i], x_recv.at[j], here.plane[i])
        return 0

    lax.fori_loop(0, n_z, forward, 0)

    def put(z, which):
        at = pl.ds(pl.multiple_of(z * block, block), block)
        dc_out[at, pl.ds(pl.multiple_of(which * LANES, LANES), LANES)] = flip[which, z]

    def cross(j, _):
        z = near_first(j)
        wait_bytes(full.at[z, pl.ds(0, n_plane - 1)], x_recv.at[j])
        flip[mine, z] = jnp.transpose(full[z].reshape(LANES, block))
        held = flip.at[mine, z]
        send(held, held, d_send.at[j], d_recv.at[j], here.partner)
        put(z, mine)
        return 0

    lax.fori_loop(0, n_z, cross, 0)

    wait_bytes(lz.at[pl.ds(0, n_z - 1)], l_recv.at[2])
    loss_out[...] = jnp.sum(lz[...], axis=0)

    def finish(j, _):
        z = near_first(j)
        wait_bytes(flip.at[other, z], d_recv.at[j])
        put(z, other)
        wait_bytes(flip.at[mine, z], d_send.at[j])
        wait_bytes(inbox.at[z], c_send.at[j])

        @pl.when(j < n_z - 1)
        def _():
            wait_bytes(tot.at[z], t_send.at[j])

        for i in range(n_plane - 1):
            wait_bytes(tot.at[z], r_send.at[j, i])
            wait_bytes(tot.at[z], x_send.at[j, i])
        return 0

    lax.fori_loop(0, n_z, finish, 0)
    for copy in sent:
        copy.wait_send()


def whole_step(dims, view_one, view_two, protos, mask):
    rows, depth = view_one.shape
    count = protos.shape[0]
    width = count + LANES
    n_plane, n_z = dims[0] * dims[1], dims[2]
    block = count // n_z
    tile = (LANES // n_plane, block)
    vmem = pl.BlockSpec(memory_space=pltpu.VMEM)
    hbm = pl.BlockSpec(memory_space=pltpu.HBM)
    dma, mem = pltpu.SemaphoreType.DMA, pltpu.VMEM
    return pl.pallas_call(
        functools.partial(step_kernel, dims),
        out_shape=(mem((2, rows, count), F32), mem((2, rows, depth), F32), mem((count, depth), F32), mem((1, LANES), F32)),
        in_specs=[hbm] * 4,
        out_specs=(vmem,) * 4,
        scratch_shapes=[
            mem((2, rows, depth), BF16),
            mem((count, depth), BF16),
            mem((rows, depth), BF16),
            mem((rows // LANES, LANES), jnp.int32),
            mem((rows // LANES, LANES), jnp.int32),
            mem((2 * rows, 1), F32),
            mem((2, rows, 1), F32),
            mem((2, 1, count), F32),
            mem((2 * rows, count), F32),
            mem((rows, count), F32),
            mem((2, rows, count), F32),
            mem((2, rows, count), F32),
            mem((2 * rows, count), BF16),
            mem((depth, 2 * rows), BF16),
            mem((2 * n_plane, 1, width), F32),
            mem((1, width), F32),
            mem((2, n_plane, 1, width - LANES), F32),
            mem((n_z, 1, width), F32),
            mem((n_z, 1, width - LANES), F32),
            mem((2 * n_z, 1, width - LANES), F32),
            mem((n_z, 2, n_plane) + tile, F32),
            mem((n_z, n_plane) + tile, F32),
            mem((n_z, n_plane) + tile, F32),
            mem((n_plane, n_z) + tile, F32),
            mem((n_z,) + tile, F32),
            mem((n_z,) + tile, F32),
            mem((n_z, n_plane) + tile, F32),
            mem((2, n_z, block, LANES), F32),
            mem((2, 1, LANES), F32),
            mem((n_plane, 1, LANES), F32),
            mem((n_z, 1, LANES), F32),
            dma((4,)),
            dma((2,)), dma((2,)),
            dma((2 * n_plane,)), dma((1,)),
            dma((2, n_plane - 1)), dma((2,)),
            dma((3, 2 * n_z - 1)), dma((3,)),
            dma((n_z,)), dma((n_z,)),
            dma((n_z, n_plane - 1)), dma((n_z,)),
            dma((n_z,)), dma((1,)),
            dma((n_z - 1,)), dma((n_z,)),
            dma((n_z, n_plane - 1)), dma((n_z,)),
            dma((n_z,)), dma((n_z,)),
            dma((n_plane + n_z,)), dma((3,)),
        ],
        compiler_params=pltpu.CompilerParams(collective_id=0, has_side_effects=True, vmem_limit_bytes=32 << 20),
        name="whole_step",
    )(*(pltpu.with_memory_space_constraint(x, pltpu.HBM)
        for x in (view_one, view_two, protos, mask.reshape(rows // LANES, LANES))))


def deliver_kernel(q_ref, dz_ref, dc_ref, loss_ref, q1, q2, dz1, dz2, dc, loss, sem):
    loss[...] = loss_ref[:, :1]
    moves = [(q_ref.at[0], q1), (q_ref.at[1], q2), (dz_ref.at[0], dz1), (dz_ref.at[1], dz2), (dc_ref, dc)]
    copies = [pltpu.make_async_copy(src, dst, sem.at[i]) for i, (src, dst) in enumerate(moves)]
    for copy in copies:
        copy.start()
    for copy in copies:
        copy.wait()


def deliver(q, dz, dc, loss):
    vmem = pl.BlockSpec(memory_space=pltpu.VMEM)
    hbm = pl.BlockSpec(memory_space=pltpu.HBM)
    shapes = [q.shape[1:]] * 2 + [dz.shape[1:]] * 2 + [dc.shape, (1, 1)]
    return pl.pallas_call(
        deliver_kernel,
        out_shape=[jax.ShapeDtypeStruct(shape, F32) for shape in shapes],
        in_specs=[vmem] * 4,
        out_specs=[hbm] * 5 + [vmem],
        scratch_shapes=[pltpu.SemaphoreType.DMA((5,))],
        compiler_params=pltpu.CompilerParams(vmem_limit_bytes=8 << 20),
        name="deliver",
    )(q, dz, dc, loss)


def solution(mesh):
    dims = torus(mesh.size)

    def local_step(view_one, view_two, protos, valid_mask):
        q, dz, dc, loss = whole_step(dims, view_one, view_two, protos, valid_mask)
        q1, q2, dz1, dz2, dc, loss = deliver(q, dz, dc, loss)
        return q1, q2, loss[0, 0], dz1, dz2, dc

    return jax.shard_map(
        local_step,
        mesh=mesh,
        in_specs=(P("data", None), P("data", None), P(None, None), P("data")),
        out_specs=(P("data", None), P("data", None), P(), P("data", None), P("data", None), P(None, None)),
        check_vma=False,
    )
```

time: 98.2 us -> 76.9 us (0.78)
  local copies, waits for them, and re-layouts: 5.72 us -> 0 us
  matrix products: 4.65 us -> 0 us
  other arithmetic: 4.3 us -> 0 us
  between operations: 3.93 us -> 0.64 us
  Pallas kernels: 79.3 us -> 76.2 us
    dot_general x6 -> x0, matrix products: 4.65 us -> none  [the longest x1 1.33 us: local_step(): jnp.einsum('nk,nd->kd', g2, view_two, preferred_element_type=F32)]
    unnamed x15 -> x0, local copies, waits for them, and re-layouts: 4.08 us -> none
    pallas_call x2, Pallas kernels: 79.3 us -> 76.2 us  [the longest x1 73.8 us: whole_step(): pl.pallas_call(functools.partial(step_kernel, dims), out_shape=(mem((2, r...]
    reduce_sum x2 -> x0, other arithmetic: 2.24 us -> none  [the longest x1 1.13 us: local_step(): jnp.sum(q1 * logp2)]
    div x3 -> x0, other arithmetic: 1.36 us -> none  [the longest x1 0.7 us: codes(): a = 1.0 / (count * sums[v, :, :count])]
    slice x1 -> x0, local copies, waits for them, and re-layouts: 1.1 us -> none  [local_step(): valid_count = sums[0, 0, count]]
where the time goes in v2:
time: 76.9 us; the launch traced here: 76.8 us
  Pallas kernels  76.2 us (99%)
    pallas_call x1, Pallas kernels, whole_step(): pl.pallas_call(functools.partial(step_kernel, dims), out_shape=(mem((2, r...  73.8 us
    pallas_call x1, Pallas kernels, deliver(): pl.pallas_call(deliver_kernel, out_shape=[jax.ShapeDtypeStruct(shape, F32...  2.39 us

profile of v2, /device:TPU:1, one launch (start us, length us, event | category | flops | bytes accessed | tf_op | source)
XLA Modules:
  0.0 76.8 jit_solution(14909254184190314533)
XLA Ops:
  0.6 73.8 %whole_step.1 = (f32[2,256,1024]{2,1,0:T(8,128)S(1)}, f32[2,256,256]{2,1,0:T(8,128)S(1)}, f32[1024,256]{1,0:T(8,128)S(1)}, f32[1,128]{1,0:T(1,128)S(1)}) custom-call(bf16[256,256]{1,0:T(8,128)(2,1)} %z1_hbm.1, bf16[256,256]{1,0:T(8,128)(2,1)} %z2_hbm.1, bf16[1024,256]{1,0:T(8,128)(2,1)} %c_hbm.1, s32[2,128]{1,0:T(2,128)} %bitcast.2), custom_call_target="tpu_custom_call" | custom-call | tf_op jit(solution)/shard_map/whole_step/pallas_call | solution.py:386
  74.4 2.4 %deliver.1 = (f32[256,1024]{1,0:T(8,128)}, f32[256,1024]{1,0:T(8,128)}, f32[256,256]{1,0:T(8,128)}, f32[256,256]{1,0:T(8,128)}, f32[1024,256]{1,0:T(8,128)}, /*index=5*/f32[1,1]{1,0:T(1,128)}) custom-call(f32[2,256,1024]{2,1,0:T(8,128)S(1)} %get-tuple-element.16.q_ref, f32[2,256,256]{2,1,0:T(8,128)S(1)} %get-tuple-element.17.dz_ref, ...), custom_call_target="tpu_custom_call" | custom-call | tf_op jit(solution)/shard_map/deliver/pallas_call | solution.py:456

commit v3 on v2

--- a/solution.py
+++ b/solution.py
@@ -38,7 +38,6 @@
         dzs = sorted(range(1, nz), key=lambda d: -ring(d, nz))
         self.column_z = [lax.rem(self.z + d, nz) for d in dzs]
         self.column = [self.at(z, self.p, self.core) for z in self.column_z]
-        self.column_other = [self.at(z, self.p, 1 - self.core) for z in self.column_z]
         self.partner = self.at(self.z, self.p, 1 - self.core)
 
     def at(self, z, p, core):
@@ -76,10 +75,10 @@
     return jnp.transpose(jnp.broadcast_to(row, (LANES, LANES)))[:, :1]
 
 
-def step_kernel(dims, z1_hbm, z2_hbm, c_hbm, m_hbm, q_out, dz_out, dc_out, loss_out,
-                zin, cbuf, zx, m_own, ms, mcol, bcol, avec, plan, plan_other, prob, logp, grad, zt,
-                xy_first, spare, xyb, z_first, zb, zlast, part, inbox, half, rs, tot, zrs, full, flip, lpair, lxy, lz,
-                in_sem, pair_send, pair_recv, f_send, f_recv, xy_send, xy_recv, z_send, z_recv,
+def step_kernel(dims, z1_hbm, z2_hbm, c_hbm, m_hbm, q_res, dz_res, dc_res, loss_out,
+                q_out, dz_out, zin, cbuf, zx, m_own, ms, mcol, bcol, avec, plan, plan_other, prob, logp, grad, zt,
+                xy_first, spare, xyb, z_first, zb, part, inbox, half, rs, tot, zrs, full, flip, lpair, lxy, lz,
+                in_sem, out_sem, pair_send, pair_recv, f_send, f_recv, xy_send, xy_recv, z_send, z_recv,
                 c_send, c_recv, r_send, r_recv, t_send, t_recv,
                 g_send, g_recv, x_send, x_recv, d_send, d_recv, l_send, l_recv):
     here = Place(dims)
@@ -88,7 +87,7 @@
     block = protos // n_z
     mine, other = here.core, 1 - here.core
     plane_other = [here.at(here.z, p, other) for p in here.plane_p]
-    groups = here.plane + plane_other + here.column + here.column_other + [here.partner]
+    groups = here.plane + plane_other + here.column + [here.partner]
     enter(groups)
 
     loads = [pltpu.make_async_copy(z1_hbm, zin.at[0], in_sem.at[0]),
@@ -124,12 +123,11 @@
         return tuple(out)
 
     zero = jnp.zeros((8, protos), F32)
-    acc_mine, acc_other = lax.fori_loop(0, rows // LANES, fill, (zero, zero))
+    acc_mine, acc_other = lax.fori_loop(0, rows // LANES, fill, (zero, zero), unroll=True)
 
     def payload(acc):
         return jnp.concatenate([jnp.sum(acc, axis=0, keepdims=True), count], axis=1)
 
-    sent = []
     slot = here.core * n_plane + here.p
     xy_first[slot] = payload(acc_mine)
     spare[...] = payload(acc_other)
@@ -138,11 +136,11 @@
 
     held = xy_first.at[slot]
     for i in range(n_plane - 1):
-        sent.append(send(held, held, f_send.at[i], f_recv.at[0], here.plane[i]))
-        sent.append(send(spare, held, f_send.at[n_plane + i], f_recv.at[0], plane_other[i]))
-    sent.append(send(spare, held, f_send.at[n_plane - 1], f_recv.at[0], here.partner))
-    sent.append(send(zin.at[other], zx, pair_send.at[0], pair_recv.at[0], here.partner))
-    sent.append(send(m_own, ms, pair_send.at[1], pair_recv.at[1], here.partner))
+        send(held, held, f_send.at[0], f_recv.at[0], here.plane[i])
+        send(spare, held, f_send.at[0], f_recv.at[0], plane_other[i])
+    send(spare, held, f_send.at[0], f_recv.at[0], here.partner)
+    z_copy = send(zin.at[other], zx, pair_send.at[0], pair_recv.at[0], here.partner)
+    m_copy = send(m_own, ms, pair_send.at[1], pair_recv.at[1], here.partner)
 
     wait_bytes(ms, pair_recv.at[1])
     for h in range(rows // LANES):
@@ -156,49 +154,40 @@
 
     lax.fori_loop(0, rows // LANES, fill_partner, 0)
 
-    def to_column(t, value, last):
-        if not last:
-            held = (z_first if t == 0 else zb).at[here.z]
-            held[...] = value
-            for i, device in enumerate(here.column):
-                sent.append(send(held, held, z_send.at[t, i], z_recv.at[t], device))
-            return
-        slot = here.core * n_z + here.z
-        zlast[slot] = value
-        held = zlast.at[slot]
-        for i, device in enumerate(here.column + here.column_other + [here.partner]):
-            sent.append(send(held, held, z_send.at[t, i], z_recv.at[t], device))
+    def to_column(t, value):
+        held = (z_first if t == 0 else zb.at[t - 1]).at[here.z]
+        held[...] = value
+        for device in here.column:
+            send(held, held, z_send.at[t], z_recv.at[t], device)
 
     def from_column(t):
-        buf = z_first if t == 0 else zb
+        buf = z_first if t == 0 else zb.at[t - 1]
         wait_bytes(buf.at[pl.ds(0, n_z - 1)], z_recv.at[t])
         return jnp.sum(buf[...], axis=0)
 
     def to_plane(t, value):
         xyb[t, here.p] = value
         held = xyb.at[t, here.p]
-        for i, device in enumerate(here.plane):
-            sent.append(send(held, held, xy_send.at[t, i], xy_recv.at[t], device))
+        for device in here.plane:
+            send(held, held, xy_send.at[t], xy_recv.at[t], device)
 
     def from_plane(t):
         wait_bytes(xyb.at[t, pl.ds(0, n_plane - 1)], xy_recv.at[t])
         return jnp.sum(xyb[t], axis=0)
 
     def sweep(a):
-        step = 32
-
         def body(i, acc):
-            at = pl.ds(pl.multiple_of(i * step, step), step)
+            at = pl.ds(pl.multiple_of(i * LANES, LANES), LANES)
             e = plan[at, :]
             m = mcol[at, :]
             r = jnp.sum(e * a, axis=1, keepdims=True) * m + (1.0 - m)
-            return acc + jnp.sum((e * (m / r)).reshape(step // 8, 8, protos), axis=0)
-
-        acc = lax.fori_loop(0, 2 * rows // step, body, zero, unroll=2)
+            return acc + fold(e, m / r)
+
+        acc = lax.fori_loop(0, 2 * rows // LANES, body, zero, unroll=True)
         return jnp.sum(acc, axis=0, keepdims=True)
 
     wait_bytes(xy_first.at[pl.ds(0, 2 * n_plane - 1)], f_recv.at[0])
-    to_column(0, jnp.sum(xy_first[...], axis=0), False)
+    to_column(0, jnp.sum(xy_first[...], axis=0))
 
     def soften(i, _):
         at = pl.ds(pl.multiple_of(i * 32, 32), 32)
@@ -216,26 +205,27 @@
     total = from_column(0)
     valid = total[:, protos:]
     for t in (0, 1):
-        a = 1.0 / (protos * total[:, :protos])
-        to_plane(t, sweep(a))
-        if t == 0:
-            to_column(1, from_plane(0), False)
-            total = from_column(1)
-        else:
-            to_column(2, from_plane(1), True)
-    wait_bytes(zlast.at[pl.ds(0, 2 * n_z - 1)], z_recv.at[2])
-    for view in range(2):
-        avec[view] = 1.0 / (protos * jnp.sum(zlast[view * n_z:(view + 1) * n_z], axis=0))
-
-    def weigh(i, _):
-        at = pl.ds(pl.multiple_of(i * 32, 32), 32)
-        m = mcol[at, :]
-        for k, (view, plan_ref) in enumerate(((mine, plan), (other, plan_other))):
+        to_plane(t, sweep(1.0 / (protos * total[:, :protos])))
+        to_column(t + 1, from_plane(t))
+        total = from_column(t + 1)
+
+    avec[mine] = 1.0 / (protos * total)
+    a_held = avec.at[mine]
+    a_copy = send(a_held, a_held, pair_send.at[2], pair_recv.at[2], here.partner)
+
+    def weigh(k, view, plan_ref):
+        def body(i, _):
+            at = pl.ds(pl.multiple_of(i * LANES, LANES), LANES)
+            m = mcol[at, :]
             r = jnp.sum(plan_ref[at, :] * avec[view], axis=1, keepdims=True) * m + (1.0 - m)
             bcol[k, at, :] = m / r
-        return 0
-
-    lax.fori_loop(0, rows // 32, weigh, 0)
+            return 0
+
+        lax.fori_loop(0, rows // LANES, body, 0, unroll=True)
+
+    weigh(0, mine, plan)
+    wait_bytes(avec.at[other], pair_recv.at[2])
+    weigh(1, other, plan_other)
     scale = mcol[0:rows, :] * (0.5 * INV_TEMP) / valid[:, :1]
 
     def derive(j, _):
@@ -253,18 +243,26 @@
         send(part.at[z, other], inbox.at[z], c_send.at[j], c_recv.at[j], here.partner)
         return 0
 
-    lax.fori_loop(0, n_z, derive, 0)
-
     def spread(j, _):
         z = here.far_first(j)
         wait_bytes(inbox.at[z], c_recv.at[j])
         half[z] = part[z, mine] + inbox[z]
         rs[here.p, z] = half[z, here.p]
         for i in range(n_plane - 1):
-            send(half.at[z, here.plane_p[i]], rs.at[here.p, z], r_send.at[j, i], r_recv.at[j], here.plane[i])
-        return 0
-
-    lax.fori_loop(0, n_z, spread, 0)
+            send(half.at[z, here.plane_p[i]], rs.at[here.p, z], r_send.at[j], r_recv.at[j], here.plane[i])
+        return 0
+
+    lag = min(3, n_z)
+    lax.fori_loop(0, lag, derive, 0)
+
+    def both(j, _):
+        derive(j, 0)
+        return spread(j - lag, 0)
+
+    lax.fori_loop(lag, n_z, both, 0)
+    lax.fori_loop(n_z - lag, n_z, spread, 0)
+    q_copy = pltpu.make_async_copy(q_out, q_res, out_sem.at[0])
+    q_copy.start()
 
     def lose(i, acc):
         at = pl.ds(pl.multiple_of(i * 32, 32), 32)
@@ -274,7 +272,7 @@
     loss = jnp.sum(lax.fori_loop(0, rows // 32, lose, zero), keepdims=True)
     lpair[here.core] = jnp.broadcast_to(loss, (1, LANES)) * (-0.5) / valid
     lheld = lpair.at[here.core]
-    sent.append(send(lheld, lheld, l_send.at[0], l_recv.at[0], here.partner))
+    send(lheld, lheld, l_send.at[0], l_recv.at[0], here.partner)
 
     def descend(i, _):
         at = pl.ds(pl.multiple_of(i * LANES, LANES), LANES)
@@ -284,12 +282,14 @@
         return 0
 
     lax.fori_loop(0, rows // LANES, descend, 0)
+    dz_copy = pltpu.make_async_copy(dz_out, dz_res, out_sem.at[1])
+    dz_copy.start()
 
     wait_bytes(lpair.at[0], l_recv.at[0])
     lxy[here.p] = lpair[0] + lpair[1]
     lheld = lxy.at[here.p]
-    for i, device in enumerate(here.plane):
-        sent.append(send(lheld, lheld, l_send.at[1 + i], l_recv.at[1], device))
+    for device in here.plane:
+        send(lheld, lheld, l_send.at[1], l_recv.at[1], device)
 
     def gather(j, _):
         z = here.far_first(j)
@@ -306,8 +306,8 @@
     wait_bytes(lxy.at[pl.ds(0, n_plane - 1)], l_recv.at[1])
     lz[here.z] = jnp.sum(lxy[...], axis=0)
     lheld = lz.at[here.z]
-    for i, device in enumerate(here.column):
-        sent.append(send(lheld, lheld, l_send.at[n_plane + i], l_recv.at[2], device))
+    for device in here.column:
+        send(lheld, lheld, l_send.at[2], l_recv.at[2], device)
 
     zrs[here.z] = tot[here.z]
     wait_bytes(zrs.at[pl.ds(0, n_z - 1)], t_recv.at[0])
@@ -317,8 +317,8 @@
         return here.far_first(n_z - 1 - j)
 
     held = full.at[here.z, here.p]
-    for i, device in enumerate(here.column):
-        sent.append(send(held, held, g_send.at[i], g_recv.at[here.z], device))
+    for device in here.column:
+        send(held, held, g_send.at[0], g_recv.at[here.z], device)
 
     def forward(j, _):
         z = near_first(j)
@@ -329,14 +329,40 @@
             wait_bytes(held, g_recv.at[z])
 
         for i in range(n_plane - 1):
-            send(held, held, x_send.at[j, i], x_recv.at[j], here.plane[i])
+            send(held, held, x_send.at[j], x_recv.at[j], here.plane[i])
         return 0
 
     lax.fori_loop(0, n_z, forward, 0)
 
-    def put(z, which):
-        at = pl.ds(pl.multiple_of(z * block, block), block)
-        dc_out[at, pl.ds(pl.multiple_of(which * LANES, LANES), LANES)] = flip[which, z]
+    def drain(j, _):
+        z = near_first(j)
+        wait_bytes(inbox.at[z], c_send.at[j])
+        wait_bytes(half.at[z, pl.ds(0, n_plane - 1)], r_send.at[j])
+
+        @pl.when(j < n_z - 1)
+        def _():
+            wait_bytes(tot.at[z], t_send.at[j])
+
+        return 0
+
+    lax.fori_loop(0, n_z, drain, 0)
+    z_copy.wait_send()
+    m_copy.wait_send()
+    a_copy.wait_send()
+    wait_bytes(xy_first.at[pl.ds(0, 2 * n_plane - 1)], f_send.at[0])
+    wait_bytes(z_first.at[pl.ds(0, n_z - 1)], z_send.at[0])
+    for t in (0, 1):
+        wait_bytes(xyb.at[t, pl.ds(0, n_plane - 1)], xy_send.at[t])
+        wait_bytes(zb.at[t, pl.ds(0, n_z - 1)], z_send.at[t + 1])
+    q_copy.wait()
+    dz_copy.wait()
+
+    def hand_over(j, which):
+        z = near_first(j)
+        return pltpu.make_async_copy(
+            flip.at[which, z],
+            dc_res.at[pl.ds(pl.multiple_of(z * block, block), block), pl.ds(pl.multiple_of(which * LANES, LANES), LANES)],
+            out_sem.at[2 + which * n_z + j])
 
     def cross(j, _):
         z = near_first(j)
@@ -344,33 +370,34 @@
         flip[mine, z] = jnp.transpose(full[z].reshape(LANES, block))
         held = flip.at[mine, z]
         send(held, held, d_send.at[j], d_recv.at[j], here.partner)
-        put(z, mine)
+        hand_over(j, mine).start()
         return 0
 
     lax.fori_loop(0, n_z, cross, 0)
 
     wait_bytes(lz.at[pl.ds(0, n_z - 1)], l_recv.at[2])
     loss_out[...] = jnp.sum(lz[...], axis=0)
+    wait_bytes(lpair.at[0], l_send.at[0])
+    wait_bytes(lxy.at[pl.ds(0, n_plane - 1)], l_send.at[1])
+    wait_bytes(lz.at[pl.ds(0, n_z - 1)], l_send.at[2])
+    wait_bytes(full.at[0, pl.ds(0, n_z - 1)], g_send.at[0])
 
     def finish(j, _):
         z = near_first(j)
         wait_bytes(flip.at[other, z], d_recv.at[j])
-        put(z, other)
+        hand_over(j, other).start()
+        wait_bytes(half.at[z, pl.ds(0, n_plane - 1)], x_send.at[j])
         wait_bytes(flip.at[mine, z], d_send.at[j])
-        wait_bytes(inbox.at[z], c_send.at[j])
-
-        @pl.when(j < n_z - 1)
-        def _():
-            wait_bytes(tot.at[z], t_send.at[j])
-
-        for i in range(n_plane - 1):
-            wait_bytes(tot.at[z], r_send.at[j, i])
-            wait_bytes(tot.at[z], x_send.at[j, i])
+        hand_over(j, mine).wait()
         return 0
 
     lax.fori_loop(0, n_z, finish, 0)
-    for copy in sent:
-        copy.wait_send()
+
+    def settle(j, _):
+        hand_over(j, other).wait()
+        return 0
+
+    lax.fori_loop(0, n_z, settle, 0)
 
 
 def whole_step(dims, view_one, view_two, protos, mask):
@@ -382,13 +409,16 @@
     tile = (LANES // n_plane, block)
     vmem = pl.BlockSpec(memory_space=pltpu.VMEM)
     hbm = pl.BlockSpec(memory_space=pltpu.HBM)
+    anywhere = pl.BlockSpec(memory_space=pl.ANY)
     dma, mem = pltpu.SemaphoreType.DMA, pltpu.VMEM
     return pl.pallas_call(
         functools.partial(step_kernel, dims),
         out_shape=(mem((2, rows, count), F32), mem((2, rows, depth), F32), mem((count, depth), F32), mem((1, LANES), F32)),
         in_specs=[hbm] * 4,
-        out_specs=(vmem,) * 4,
+        out_specs=(anywhere,) * 3 + (vmem,),
         scratch_shapes=[
+            mem((2, rows, count), F32),
+            mem((2, rows, depth), F32),
             mem((2, rows, depth), BF16),
             mem((count, depth), BF16),
             mem((rows, depth), BF16),
@@ -407,8 +437,7 @@
             mem((1, width), F32),
             mem((2, n_plane, 1, width - LANES), F32),
             mem((n_z, 1, width), F32),
-            mem((n_z, 1, width - LANES), F32),
-            mem((2 * n_z, 1, width - LANES), F32),
+            mem((2, n_z, 1, width - LANES), F32),
             mem((n_z, 2, n_plane) + tile, F32),
             mem((n_z, n_plane) + tile, F32),
             mem((n_z, n_plane) + tile, F32),
@@ -420,18 +449,18 @@
             mem((2, 1, LANES), F32),
             mem((n_plane, 1, LANES), F32),
             mem((n_z, 1, LANES), F32),
-            dma((4,)),
+            dma((4,)), dma((2 + 2 * n_z,)),
+            dma((3,)), dma((3,)),
+            dma((1,)), dma((1,)),
             dma((2,)), dma((2,)),
-            dma((2 * n_plane,)), dma((1,)),
-            dma((2, n_plane - 1)), dma((2,)),
-            dma((3, 2 * n_z - 1)), dma((3,)),
+            dma((3,)), dma((3,)),
             dma((n_z,)), dma((n_z,)),
-            dma((n_z, n_plane - 1)), dma((n_z,)),
+            dma((n_z,)), dma((n_z,)),
             dma((n_z,)), dma((1,)),
-            dma((n_z - 1,)), dma((n_z,)),
-            dma((n_z, n_plane - 1)), dma((n_z,)),
+            dma((1,)), dma((n_z,)),
             dma((n_z,)), dma((n_z,)),
-            dma((n_plane + n_z,)), dma((3,)),
+            dma((n_z,)), dma((n_z,)),
+            dma((3,)), dma((3,)),
         ],
         compiler_params=pltpu.CompilerParams(collective_id=0, has_side_effects=True, vmem_limit_bytes=32 << 20),
         name="whole_step",
@@ -456,7 +485,7 @@
     return pl.pallas_call(
         deliver_kernel,
         out_shape=[jax.ShapeDtypeStruct(shape, F32) for shape in shapes],
-        in_specs=[vmem] * 4,
+        in_specs=[pl.BlockSpec(memory_space=pl.ANY)] * 3 + [vmem],
         out_specs=[hbm] * 5 + [vmem],
         scratch_shapes=[pltpu.SemaphoreType.DMA((5,))],
         compiler_params=pltpu.CompilerParams(vmem_limit_bytes=8 << 20),

time: 76.9 us -> 70 us (0.910)
  Pallas kernels: 76.2 us -> 69.2 us
    pallas_call x1, Pallas kernels: 73.8 us -> 66.8 us  [whole_step(): pl.pallas_call(functools.partial(step_kernel, dims), out_shape=(mem((2, r...]
where the time goes in v3:
time: 70 us; the launch traced here: 69.9 us
  Pallas kernels  69.2 us (99%)
    pallas_call x1, Pallas kernels, whole_step(): pl.pallas_call(functools.partial(step_kernel, dims), out_shape=(mem((2, r...  66.8 us
    pallas_call x1, Pallas kernels, deliver(): pl.pallas_call(deliver_kernel, out_shape=[jax.ShapeDtypeStruct(shape, F32...  2.39 us

profile of v3, /device:TPU:1, one launch (start us, length us, event | category | flops | bytes accessed | tf_op | source)
XLA Modules:
  0.0 69.9 jit_solution(13216430301142999221)
XLA Ops:
  0.6 66.8 %whole_step.1 = (f32[2,256,1024]{2,1,0:T(8,128)S(1)}, f32[2,256,256]{2,1,0:T(8,128)S(1)}, f32[1024,256]{1,0:T(8,128)S(1)}, f32[1,128]{1,0:T(1,128)S(1)}) custom-call(bf16[256,256]{1,0:T(8,128)(2,1)} %z1_hbm.1, bf16[256,256]{1,0:T(8,128)(2,1)} %z2_hbm.1, bf16[1024,256]{1,0:T(8,128)(2,1)} %c_hbm.1, s32[2,128]{1,0:T(2,128)} %bitcast.2), custom_call_target="tpu_custom_call" | custom-call | tf_op jit(solution)/shard_map/whole_step/pallas_call | solution.py:414
  67.5 2.4 %deliver.1 = (f32[256,1024]{1,0:T(8,128)}, f32[256,1024]{1,0:T(8,128)}, f32[256,256]{1,0:T(8,128)}, f32[256,256]{1,0:T(8,128)}, f32[1024,256]{1,0:T(8,128)}, /*index=5*/f32[1,1]{1,0:T(1,128)}) custom-call(f32[2,256,1024]{2,1,0:T(8,128)S(1)} %get-tuple-element.16.q_ref, f32[2,256,256]{2,1,0:T(8,128)S(1)} %get-tuple-element.17.dz_ref, ...), custom_call_target="tpu_custom_call" | custom-call | tf_op jit(solution)/shard_map/deliver/pallas_call | solution.py:485
